TPU v7x, 256 devices: a whole 4x4x8 slice. The times are simulated.
256 devices in a mesh: blk: 128 (over z, x, y_lo, core), rep: 2 (over y_hi).
Axes of the slice: x: 4, y: 4 (y_hi: 2, y_lo: 2; y = y_hi * 2 + y_lo), z: 8, core: 2. Of those that a mesh axis runs over, the one named last changes fastest.
Arguments:
- particles: bfloat16 [7168, 2048], P(('blk', 'rep')), may hold values from -0.0029907227 to 0.0029907227
- scores: bfloat16 [7168, 2048], P(('blk', 'rep')), may hold values from -60 to 60, as said below
- spread: float32 [1], replicated, may hold values from 0.00034816 to 0.00069632
Outputs:
- direction: float32 [7168, 2048], P(('blk', 'rep'))
Inputs may be any that keep to these rules, and one draw needn't show every extreme that they name: `scores`: scores of the particles' log posterior.
All inputs are finite; a program needn't handle non-finite values.
Results may differ from a plain program's by a relative error of at most 0.0003.
Values may be sent and summed in bfloat16 or wider, within the bound.
No kernel may reach another device: no remote copies, remote signals or barrier semaphores. Data moves between devices by JAX's collectives and lax.ppermute only.
A program may use at most 128 MiB of HBM per device.

v0:
```python
import jax
import jax.numpy as jnp
from jax import lax
from jax.sharding import PartitionSpec as P


def sent_to_all(value, axis):
    count = lax.axis_size(axis)
    return lax.all_to_all(
        jnp.broadcast_to(value[None], (count, *value.shape)), axis, 0, 0, tiled=True
    )


def joined_along(blocks, dim):
    dims = list(blocks.shape[1:])
    dims[dim] *= blocks.shape[0]
    return jnp.moveaxis(blocks, 0, dim).reshape(dims)


def gather_directly(value, axis, dim):
    blocks = sent_to_all(value, axis)
    return joined_along(blocks, dim)


def in_blocks(value, dim, count):
    before, after = (value.shape[:dim], value.shape[dim + 1 :])
    return jnp.moveaxis(value.reshape(*before, count, -1, *after), dim, 0)


def summed_on_arrival(value, axis, dim):
    blocks = in_blocks(value, dim, lax.axis_size(axis))
    arrived = lax.all_to_all(blocks, axis, split_axis=0, concat_axis=0, tiled=True)
    return arrived.sum(axis=0)


def kernel_weights(targets, target_norm, source_x, inverse):
    cross_dots = lax.dot_general(
        targets, source_x, (((1,), (1,)), ((), ())), preferred_element_type=jnp.float32
    )
    source_wide = source_x.astype(jnp.float32)
    source_norm = jnp.sum(source_wide * source_wide, axis=1)
    squared = jnp.maximum(target_norm[:, None] + source_norm[None, :] - 2.0 * cross_dots, 0.0)
    return jnp.exp(-squared * inverse)


def shards(particles, scores, spread):
    inverse = 1.0 / spread[0]
    own_count = particles.shape[0]
    population = own_count * lax.axis_size("blk") * lax.axis_size("rep")
    targets = gather_directly(particles, "rep", 0)
    target_wide = targets.astype(jnp.float32)
    target_norm = jnp.sum(target_wide * target_wide, axis=1)
    stacked = jnp.stack([scores, particles], axis=0)
    source = lax.all_gather(stacked, "blk", axis=1, tiled=True)
    weights = kernel_weights(targets, target_norm, source[1], inverse)
    weights_low = weights.astype(jnp.bfloat16)
    combined_step = jnp.einsum(
        "ij,cjd->cid", weights_low, source, preferred_element_type=jnp.float32
    )
    row_total = jnp.sum(weights, axis=1)
    drive_sum = combined_step[0]
    pull_sum = combined_step[1]
    partial_value = (
        drive_sum + 2.0 * inverse * (target_wide * row_total[:, None] - pull_sum)
    ) / population
    return summed_on_arrival(partial_value, "rep", 0)


def solution(mesh):
    return jax.shard_map(
        shards,
        mesh=mesh,
        in_specs=(P(("blk", "rep"), None), P(("blk", "rep"), None), P()),
        out_specs=P(("blk", "rep"), None),
        check_vma=False,
    )
```

profile of v0, /device:TPU:32, one launch (start us, length us, event | category | flops | bytes accessed | tf_op | source)
XLA Modules:
  0.0 333.5 jit_solution(15019230798505263982)
XLA Ops:
  6.5 0.0 all-gather.2.cloned.1.call-start
  6.5 1.0 pad_maximum_fusion
  7.5 0.9 copy.5
  8.5 0.0 all-gather.2.cloned.1.call-update
  8.5 1.6 broadcast_in_dim.2
  10.1 4.5 %all-to-all-start = ((bf16[2,28,2048]{2,1,0:T(8,128)(2,1)}), bf16[2,28,2048]{2,1,0:T(8,128)(2,1)S(1)}, u32[]{:S(2)}, u32[]{:S(2)}) async-start(bf16[2,28,2048]{2,1,0:T(8,128)(2,1)} %broadcast_in_dim.2), calls=%async_computation | async-start | bytes 524288 | tf_op jit(solution)/shard_map/all_to_all | solution.py:9
  15.3 6.0 %all-to-all-done = bf16[2,28,2048]{2,1,0:T(8,128)(2,1)S(1)} async-done(((bf16[2,28,2048]{2,1,0:T(8,128)(2,1)}), bf16[2,28,2048]{2,1,0:T(8,128)(2,1)S(1)}, u32[]{:S(2)}, u32[]{:S(2)}) %all-to-all-start) | async-done | bytes 229408 | tf_op jit(solution)/shard_map/all_to_all | solution.py:9
  21.3 0.1 fusion.8
  21.4 0.1 add.19
  21.5 0.1 reshape.19
  21.5 235.9 %all-gather.2.cloned.1.call-done = bf16[2,3584,2048]{2,0,1:T(2,128)(2,1)} async-done(((bf16[2,28,2048]{2,0,1:T(2,128)(2,1)}), bf16[2,3584,2048]{2,0,1:T(2,128)(2,1)}) %all-gather.2.cloned.1.call-update) | async-done | bytes 29360144 | tf_op jit(solution)/shard_map/all_gather | solution.py:54
  257.4 20.5 %copy.7 = bf16[2,3584,2048]{2,1,0:T(8,128)(2,1)} copy(bf16[2,3584,2048]{2,0,1:T(2,128)(2,1)} %all-gather.2.cloned.1.call-done) | data formatting | bytes 58720256 | tf_op jit(solution)/shard_map/all_gather | solution.py:54
  277.9 8.1 %multiply_reduce_fusion = f32[3584]{0:T(1024)S(1)} fusion(bf16[2,3584,2048]{2,1,0:T(8,128)(2,1)} %copy.7), kind=kLoop, calls=%fused_computation | loop fusion | flops 22016512 | bytes 14694400 | tf_op jit(solution)/shard_map/reduce_sum | solution.py:41
  286.0 8.2 %fusion.17 = (f32[56]{0:T(128)S(1)}, bf16[56,3584]{1,0:T(8,128)(2,1)S(1)}) fusion(f32[]{:T(128)} %bitcast.4, bf16[56,2048]{1,0:T(8,128)(2,1)S(1)} %reshape.19, bf16[2,3584,2048]{2,1,0:T(8,128)(2,1)} %copy.7, f32[3584]{0:T(1024)S(1)} %multiply_reduce_fusion, f32[56]{0:T(128)S(1)} %add.19), kind=kOutput, calls=%fused_computation.23 | convolution fusion | flops 823689152 | bytes 15326144 | tf_op jit(solution)/shard_map/dot_general | solution.py:37
  294.2 18.1 %convolution_bitcast_fusion = f32[2,56,2048]{2,1,0:T(8,128)S(1)} fusion(bf16[56,3584]{1,0:T(8,128)(2,1)S(1)} %get-tuple-element.8, bf16[2,3584,2048]{2,0,1:T(2,128)(2,1)} %all-gather.2.cloned.1.call-done), kind=kOutput, calls=%fused_computation.10 | convolution fusion | flops 1644167168 | bytes 30679040 | tf_op jit(solution)/shard_map/ij,cjd->cid/dot_general | solution.py:57
  312.4 0.1 fusion.16
  312.5 0.1 mul.52
  312.6 0.2 fusion.12
  312.8 13.1 %all_to_all.10 = f32[2,28,2048]{2,1,0:T(8,128)S(1)} all-to-all(f32[2,28,2048]{2,1,0:T(8,128)S(1)} %fusion.12), channel_id=1, replica_groups=mesh['blk'=128,'rep'=2] {'rep'}, dimensions={0} | all-to-all | bytes 917504 | tf_op jit(solution)/shard_map/all_to_all | solution.py:32
  325.9 0.7 reduce_sum.39
  (2 shorter events, 0.1 us)
Async XLA Ops:
  6.5 250.9 %all-gather.2.cloned.1.call-start = ((), (), s32[]{:S(2)}) async-start(), calls=%async_computation.2 | async-start | bytes 29589504 | tf_op jit(solution)/shard_map/all_gather | solution.py:54
  10.1 11.1 %all-to-all-start = ((bf16[2,28,2048]{2,1,0:T(8,128)(2,1)}), bf16[2,28,2048]{2,1,0:T(8,128)(2,1)S(1)}, u32[]{:S(2)}, u32[]{:S(2)}) async-start(bf16[2,28,2048]{2,1,0:T(8,128)(2,1)} %broadcast_in_dim.2), calls=%async_computation | async-start | bytes 524288 | tf_op jit(solution)/shard_map/all_to_all | solution.py:9
Sparse Core Ops, SparseCore 0:
  9.2 248.1 all-gather.1
where the time goes:
time: 334 us
  waiting for transfers between devices  242 us (72%)
  matrix products  26.3 us (8%)
  local copies, waits for them, and re-layouts  23.5 us (7%)
  between operations  14.1 us (4%)
  blocking collectives  13.1 us (4%)
  other arithmetic  10.1 us (3%)
  starting transfers between devices  4.46 us (1%)
    all_gather x1, waiting for transfers between devices, shards(): source = lax.all_gather(stacked, 'blk', axis=1, tiled=True)  236 us
    all_gather x1, local copies, waits for them, and re-layouts, shards(): source = lax.all_gather(stacked, 'blk', axis=1, tiled=True)  20.5 us
    dot_general x1, matrix products, shards(): jnp.einsum('ij,cjd->cid', weights_low, source, preferred_element_type=jnp...  18.1 us
    all_to_all x1, blocking collectives, summed_on_arrival(): lax.all_to_all(blocks, axis, split_axis=0, concat_axis=0, tiled=True)  13.1 us
    dot_general x1, matrix products, kernel_weights(): lax.dot_general(targets, source_x, (((1,), (1,)), ((), ())), preferred_el...  8.21 us
    reduce_sum x1, other arithmetic, kernel_weights(): source_norm = jnp.sum(source_wide * source_wide, axis=1)  8.09 us
  transfers between devices with their start and end apart: 2, of which 2 were waited for; matrix products, arithmetic and copies ran while one was open for 1% of the time, Pallas kernels for 0%

commit v1 on v0

--- a/solution.py
+++ b/solution.py
@@ -51,7 +51,8 @@
     target_wide = targets.astype(jnp.float32)
     target_norm = jnp.sum(target_wide * target_wide, axis=1)
     stacked = jnp.stack([scores, particles], axis=0)
-    source = lax.all_gather(stacked, "blk", axis=1, tiled=True)
+    sent = jnp.stack([stacked] * lax.axis_size("blk"))
+    source = jnp.concatenate(lax.all_to_all(sent, "blk", 0, 0), axis=1)
     weights = kernel_weights(targets, target_norm, source[1], inverse)
     weights_low = weights.astype(jnp.bfloat16)
     combined_step = jnp.einsum(

time: 334 us -> 930 us (2.78)
  waiting for transfers between devices: 242 us -> 671 us
  local copies, waits for them, and re-layouts: 23.5 us -> 137 us
  other arithmetic: 10.1 us -> 56.8 us
  between operations: 14.1 us -> 0.76 us
  starting transfers between devices: 4.46 us -> 17.5 us
    all_to_all x0 -> x1, waiting for transfers between devices: none -> 666 us  [shards(): source = jnp.concatenate(lax.all_to_all(sent, 'blk', 0, 0), axis=1)]
    all_gather x1 -> x0, waiting for transfers between devices: 236 us -> none  [shards(): source = lax.all_gather(stacked, 'blk', axis=1, tiled=True)]
    slice x0 -> x1, local copies, waits for them, and re-layouts: none -> 97.2 us  [shards(): weights = kernel_weights(targets, target_norm, source[1], inverse)]
    reduce_sum x1, other arithmetic: 8.09 us -> 54.7 us  [kernel_weights(): source_norm = jnp.sum(source_wide * source_wide, axis=1)]
    squeeze x0 -> x1, local copies, waits for them, and re-layouts: none -> 20.6 us  [shards(): weights = kernel_weights(targets, target_norm, source[1], inverse)]
    all_gather x1 -> x0, local copies, waits for them, and re-layouts: 20.5 us -> none  [shards(): source = lax.all_gather(stacked, 'blk', axis=1, tiled=True)]
    another operation x0 -> x1, local copies, waits for them, and re-layouts: none -> 17.3 us  [shards(): sent = jnp.stack([stacked] * lax.axis_size('blk'))]
    all_to_all x0 -> x1, starting transfers between devices: none -> 13 us  [shards(): source = jnp.concatenate(lax.all_to_all(sent, 'blk', 0, 0), axis=1)]
  transfers between devices with their start and end apart: 2 -> 2, of which waited for: 2 -> 2; matrix products, arithmetic and copies ran while one was open for 1% -> 0% of each run, Pallas kernels for 0% -> 0%
where the time goes in v1:
time: 930 us; the launch traced here: 924 us
  waiting for transfers between devices  671 us (72%)
  local copies, waits for them, and re-layouts  137 us (15%)
  other arithmetic  56.8 us (6%)
  matrix products  28.1 us (3%)
  starting transfers between devices  17.5 us (2%)
  blocking collectives  11.9 us (1%)
    all_to_all x1, waiting for transfers between devices, shards(): source = jnp.concatenate(lax.all_to_all(sent, 'blk', 0, 0), axis=1)  666 us
    slice x1, local copies, waits for them, and re-layouts, shards(): weights = kernel_weights(targets, target_norm, source[1], inverse)  97.2 us
    reduce_sum x1, other arithmetic, kernel_weights(): source_norm = jnp.sum(source_wide * source_wide, axis=1)  54.7 us
    squeeze x1, local copies, waits for them, and re-layouts, shards(): weights = kernel_weights(targets, target_norm, source[1], inverse)  20.6 us
  transfers between devices with their start and end apart: 2, of which 2 were waited for; matrix products, arithmetic and copies ran while one was open for 0% of the time, Pallas kernels for 0%

profile of v1, /device:TPU:32, one launch (start us, length us, event | category | flops | bytes accessed | tf_op | source)
XLA Modules:
  0.0 923.7 jit_solution(2775050105584541709)
XLA Ops:
  0.0 1.6 broadcast_in_dim.2
  1.6 4.5 all-to-all-start.1
  6.1 1.0 pad_maximum_fusion
  7.1 0.2 copy.6
  7.3 5.4 all-to-all-done.1
  12.8 17.3 %stack.11 = bf16[128,2,28,2048]{3,1,2,0:T(2,128)(2,1)} broadcast(bf16[2,28,2048]{2,0,1:T(2,128)(2,1)S(1)} %copy.6), dimensions={1,2,3} | broadcast | bytes 29589504 | tf_op jit(solution)/shard_map/stack | solution.py:54
  30.1 13.0 %all-to-all-start = ((bf16[128,2,28,2048]{3,1,2,0:T(2,128)(2,1)}), bf16[128,2,28,2048]{3,1,2,0:T(2,128)(2,1)}, u32[]{:S(2)}, u32[]{:S(2)}) async-start(bf16[128,2,28,2048]{3,1,2,0:T(2,128)(2,1)} %stack.11), calls=%async_computation | async-start | bytes 58720256 | tf_op jit(solution)/shard_map/all_to_all | solution.py:55
  43.8 0.1 fusion.11
  44.0 0.1 add.21
  44.0 0.1 reshape.33
  44.1 666.0 %all-to-all-done = bf16[128,2,28,2048]{3,1,2,0:T(2,128)(2,1)} async-done(((bf16[128,2,28,2048]{3,1,2,0:T(2,128)(2,1)}), bf16[128,2,28,2048]{3,1,2,0:T(2,128)(2,1)}, u32[]{:S(2)}, u32[]{:S(2)}) %all-to-all-start) | async-done | bytes 29360160 | tf_op jit(solution)/shard_map/all_to_all | solution.py:55
  710.1 97.2 %slice_reduce_fusion = bf16[128,28,2048]{2,1,0:T(8,128)(2,1)} fusion(bf16[2,128,28,2048]{3,0,2,1:T(2,128)(2,1)} %bitcast.2), kind=kLoop, calls=%fused_computation.3 | loop fusion | bytes 29360128 | tf_op jit(solution)/shard_map/slice | solution.py:56
  807.2 54.7 %multiply_reduce_fusion = f32[128,28]{1,0:T(8,128)S(1)} fusion(bf16[2,128,28,2048]{3,0,2,1:T(2,128)(2,1)} %bitcast.2), kind=kLoop, calls=%fused_computation.2 | loop fusion | flops 22016512 | bytes 14694400 | tf_op jit(solution)/shard_map/reduce_sum | solution.py:41
  861.9 20.6 %squeeze.10 = bf16[3584,2048]{1,0:T(8,128)(2,1)} reshape(bf16[128,28,2048]{2,1,0:T(8,128)(2,1)} %slice_reduce_fusion) | data formatting | bytes 29360128 | tf_op jit(solution)/shard_map/squeeze | solution.py:56
  882.5 0.1 add.23
  882.6 9.9 %fusion.19 = (f32[56]{0:T(128)S(1)}, bf16[56,3584]{1,0:T(8,128)(2,1)S(1)}) fusion(f32[]{:T(128)} %bitcast.5, bf16[3584,2048]{1,0:T(8,128)(2,1)} %squeeze.10, bf16[56,2048]{1,0:T(8,128)(2,1)S(1)} %reshape.33, f32[3584]{0:T(1024)S(1)} %add.23, f32[56]{0:T(128)S(1)} %add.21), kind=kOutput, calls=%fused_computation.23 | convolution fusion | flops 823689152 | bytes 15325636 | tf_op jit(solution)/shard_map/dot_general | solution.py:37
  892.5 18.2 %fusion.8 = f32[2,56,2048]{2,1,0:T(8,128)S(1)} fusion(bf16[2,3584,2048]{2,0,1:T(2,128)(2,1)} %bitcast.3, bf16[56,3584]{1,0:T(8,128)(2,1)S(1)} %get-tuple-element.8), kind=kOutput, calls=%fused_computation.11 | convolution fusion | flops 1644167168 | bytes 30679040 | tf_op jit(solution)/shard_map/ij,cjd->cid/dot_general | solution.py:58
  910.7 0.1 fusion.18
  910.9 0.1 mul.53
  910.9 0.2 fusion.15
  911.1 11.9 %all_to_all.15 = f32[2,28,2048]{2,1,0:T(8,128)S(1)} all-to-all(f32[2,28,2048]{2,1,0:T(8,128)S(1)} %fusion.15), channel_id=1, replica_groups=mesh['blk'=128,'rep'=2] {'rep'}, dimensions={0} | all-to-all | bytes 917504 | tf_op jit(solution)/shard_map/all_to_all | solution.py:32
  923.0 0.7 reduce_sum.39
  (2 shorter events, 0.1 us)
Async XLA Ops:
  1.6 11.1 %all-to-all-start.1 = ((bf16[2,28,2048]{2,1,0:T(8,128)(2,1)}), bf16[2,28,2048]{2,1,0:T(8,128)(2,1)S(1)}, u32[]{:S(2)}, u32[]{:S(2)}) async-start(bf16[2,28,2048]{2,1,0:T(8,128)(2,1)} %broadcast_in_dim.2), calls=%async_computation.1 | async-start | bytes 524288 | tf_op jit(solution)/shard_map/all_to_all | solution.py:9
  30.1 680.0 %all-to-all-start = ((bf16[128,2,28,2048]{3,1,2,0:T(2,128)(2,1)}), bf16[128,2,28,2048]{3,1,2,0:T(2,128)(2,1)}, u32[]{:S(2)}, u32[]{:S(2)}) async-start(bf16[128,2,28,2048]{3,1,2,0:T(2,128)(2,1)} %stack.11), calls=%async_computation | async-start | bytes 58720256 | tf_op jit(solution)/shard_map/all_to_all | solution.py:55
